TPU v7x, 512 devices: a whole 4x4x16 slice. The times are simulated.
512 devices in a mesh: seq: 128 (over z_lo, y, x), tp: 4 (over z_hi, core).
Axes of the slice: x: 4, y: 4, z: 16 (z_hi: 2, z_lo: 8; z = z_hi * 8 + z_lo), core: 2. Of those that a mesh axis runs over, the one named last changes fastest.
Arguments:
- inputs: bfloat16 [32768, 5120], P('seq', 'tp'), may hold values from -6 to 6
- gate_input: bfloat16 [32768, 5120], P('seq', 'tp'), may hold values from -6 to 6
- b_source: bfloat16 [32768, 128], P('seq'), may hold values from -6 to 6
- c_source: bfloat16 [32768, 128], P('seq'), may hold values from -6 to 6
- step_raw: float32 [32768, 80], P('seq', 'tp'), may hold values from -4 to 4
- step_bias: float32 [80], P('tp'), may hold values from -3 to 0
- decay_rate: float32 [80], P('tp'), may hold values from 6.1035157e-06 to 0.05
- conv_weight: float32 [4, 256], replicated, may hold values from -3 to 3
- conv_bias: float32 [256], replicated, may hold values from -3 to 3
- norm_gain: float32 [5120], P('tp'), may hold values from 0.5 to 1.5
- doc_lengths: int32 [8], replicated, may hold values from 1 to 16384, 32768 in all
Outputs:
- output: bfloat16 [32768, 5120], P('seq', 'tp')
Inputs may be any that keep to these rules, and one draw needn't show every extreme that they name: doc_lengths sums to 32768; every length is at least 1 and the largest is exactly 16384.
All inputs are finite; a program needn't handle non-finite values.
Results may differ from a plain program's by a relative error of at most 0.0015.
Values may be sent and summed in bfloat16 or wider, within the bound.
No kernel may reach another device: no remote copies, remote signals or barrier semaphores. Data moves between devices by JAX's collectives and lax.ppermute only.
A program may use at most 192 MiB of HBM per device.

v0:
```python
import functools

import jax
import jax.numpy as jnp
from jax import lax
from jax.experimental import pallas as pl
from jax.experimental.pallas import tpu as pltpu
from jax.sharding import Mesh
from jax.sharding import PartitionSpec as P

SEQ = ("za", "zb", "y", "x")
GROUP = ("zb", "y", "x")
OUTER = "za"
LANES = 128
epsilon = 1e-05
VMEM = pl.BlockSpec(memory_space=pltpu.VMEM)
HBM = pl.BlockSpec(memory_space=pltpu.HBM)


def call(
    kernel, outs, *args, hbm=0, after=(), scratch=(), flops=1_000_000, aliases=None, to_hbm=False
):
    if after:
        inner, skip = kernel, len(after)
        kernel = lambda *refs: inner(*refs[:len(args)], *refs[len(args) + skip:])
    multiple = isinstance(outs, (list, tuple))
    return pl.pallas_call(
        kernel,
        out_shape=list(outs) if multiple else outs,
        in_specs=[HBM] * hbm + [VMEM] * (len(args) - hbm) + [VMEM] * len(after),
        out_specs=[VMEM] * len(outs) if multiple else HBM if to_hbm else VMEM,
        input_output_aliases=aliases or {},
        scratch_shapes=list(scratch),
        compiler_params=pltpu.CompilerParams(vmem_limit_bytes=24 * 1024 * 1024),
        cost_estimate=pl.CostEstimate(flops=flops, bytes_accessed=1_000_000, transcendentals=0),
    )(*(pltpu.with_memory_space_constraint(a, pltpu.HBM) for a in args[:hbm]), *args[hbm:], *after)


def out(shape, dtype=jnp.float32):
    return pltpu.VMEM(shape, dtype)


def tile_of_heads(columns, tile, width):
    per, rows = LANES // width, columns.shape[0]
    lane = lax.broadcasted_iota(jnp.int32, (rows, LANES), 1)
    h = tile * per
    spread = jnp.broadcast_to(columns[:, h : h + 1], (rows, LANES))
    for k in range(1, per):
        other = jnp.broadcast_to(columns[:, h + k : h + k + 1], (rows, LANES))
        spread = jnp.where(lane < k * width, spread, other)
    return spread


def tails_kernel(b_ref, c_ref, *refs):
    count = (len(refs) - 2) // 2
    sources, tails_ref, targets, sems = refs[:count], refs[count], refs[count + 1 : -1], refs[-1]
    tokens, state = b_ref.shape
    copies = [
        pltpu.make_async_copy(
            r.at[pl.ds(tokens - 8, 8), :], tails_ref.at[:, pl.ds(k * state, state)], sems.at[k]
        )
        for k, r in enumerate((b_ref, c_ref))
    ]
    for k, (source, target) in enumerate(zip(sources, targets)):
        copies.append(pltpu.make_async_copy(source, target, sems.at[k + 2]))
    for copy in copies:
        copy.start()
    for copy in copies:
        copy.wait()


def convolve(padded_ref, weight, bias, relative, start):
    tokens = relative.shape[0]
    taps = weight.shape[0]
    summed = jnp.broadcast_to(bias, (tokens, bias.shape[1]))
    for k in range(taps):
        back = taps - 1 - k
        term = weight[k : k + 1, :] * padded_ref[8 - back : 8 - back + tokens, :]
        summed = summed + jnp.where(relative - back >= start, term, 0.0)
    return (summed * jax.nn.sigmoid(summed)).astype(jnp.bfloat16)


def bf16_parts(value):
    parts = []
    for _ in range(3):
        part = value.astype(jnp.bfloat16)
        parts.append(part)
        value = value - part.astype(jnp.float32)
    return parts


def spread_matrix(first, last, width, at):
    row = lax.broadcasted_iota(jnp.int32, (LANES, last - first), 0)
    head = (first + lax.broadcasted_iota(jnp.int32, (LANES, last - first), 1)) // width
    inside = (row >= at) if at else (row < 32)
    return jnp.where(inside & ((row & 31) == head), 1.0, 0.0).astype(jnp.bfloat16)


def spread_rows(values, features, heads, wide_ref):
    count = values.shape[0]
    parts = jnp.concatenate(bf16_parts(jnp.where(
        lax.broadcasted_iota(jnp.int32, values.shape, 1) < heads, values, 0.0
    )), axis=0)
    for j in range(0, features, 256):
        wide = jnp.dot(
            parts, spread_matrix(j, j + 256, features // heads, 0),
            preferred_element_type=jnp.float32,
        )
        wide_ref[:, j : j + 256] = (
            wide[2 * count :] + wide[count : 2 * count]
        ) + wide[0:count]


def sequence_index():
    index = 0
    for axis in SEQ:
        index = index * lax.axis_size(axis) + lax.axis_index(axis)
    return index


def to_column(row):
    n = row.shape[1]
    same = lax.broadcasted_iota(jnp.int32, (n, n), 0) == lax.broadcasted_iota(jnp.int32, (n, n), 1)
    return jnp.sum(jnp.where(same, jnp.broadcast_to(row, (n, n)), 0.0), axis=1, keepdims=True)


WEIGHTS_AT = 32


def prepare_kernel(*refs):
    count, given = 2, 9
    sources, targets = refs[:count], refs[count + given : 2 * count + given]
    (
        x_ref, docs_ref, raw_ref, bias_ref, rate_ref, b_ref, taps_ref, taps_bias_ref, _,
    ) = refs[count : count + given]
    (
        weighted_ref, cum_rows_ref, step_rows_ref, columns_ref, factor_ref, start_ref, b_conv_ref,
        stack_ref, padded_ref, sems,
    ) = refs[2 * count + given :]
    copies = [
        pltpu.make_async_copy(source, target, sems.at[k])
        for k, (source, target) in enumerate(zip(sources, targets))
    ]
    for copy in copies:
        copy.start()
    heads, tokens = raw_ref.shape
    state = b_ref.shape[1]
    width = x_ref.shape[1] // heads
    base = sequence_index() * tokens
    relative = lax.broadcasted_iota(jnp.int32, (tokens, LANES), 0)
    start = jnp.zeros((1, 1), jnp.int32) - base
    last_position = jnp.full((1, 1), tokens - 1, jnp.int32)
    chosen = jnp.broadcast_to(start, relative.shape)
    end_start = start
    for i in range(1, docs_ref.shape[1]):
        start = start + docs_ref[0:1, i - 1 : i]
        chosen = jnp.where(start <= relative, start, chosen)
        end_start = jnp.where(start <= last_position, start, end_start)
    start_ref[...] = chosen

    step = jax.nn.softplus(raw_ref[...] + to_column(bias_ref[...]))
    log_decay = -step * to_column(rate_ref[...])
    rows = lax.broadcasted_iota(jnp.int32, (tokens, tokens), 0)
    cols = lax.broadcasted_iota(jnp.int32, (tokens, tokens), 1)
    upper = jnp.where(rows <= cols, 1.0, 0.0).astype(jnp.bfloat16)
    cum = sum(
        jnp.dot(part, upper, preferred_element_type=jnp.float32)
        for part in reversed(bf16_parts(log_decay))
    )
    cum_rows_ref[...] = cum
    step_rows_ref[...] = step
    position = lax.broadcasted_iota(jnp.int32, (heads, tokens), 1)
    weighting = jnp.where(
        position >= end_start, jnp.exp(cum[:, tokens - 1 : tokens] - cum) * step, 0.0
    )
    stack_ref[...] = jnp.zeros_like(stack_ref)
    stack_ref[0:heads, :] = cum
    for k, part in enumerate(bf16_parts(weighting)):
        at = WEIGHTS_AT * (k + 1)
        stack_ref[at : at + heads, :] = part.astype(jnp.float32)
    columns = stack_ref[...].T
    columns_ref[...] = columns
    factor_ref[...] = jnp.where(end_start < 0, jnp.exp(columns[tokens - 1 : tokens, :]), 0.0)
    side = slice(0, state)
    padded_ref[0:8, :] = jnp.zeros((8, state), jnp.float32)
    padded_ref[8:, :] = b_ref[...].astype(jnp.float32)
    b_conv = convolve(padded_ref, taps_ref[:, side], taps_bias_ref[:, side], relative, chosen)
    b_conv_ref[...] = b_conv.astype(jnp.float32)
    weights = columns.astype(jnp.bfloat16)
    for j in range(0, x_ref.shape[1], 256):
        tile = slice(j, j + 256)
        spread = jnp.dot(
            weights, spread_matrix(j, j + 256, width, WEIGHTS_AT),
            preferred_element_type=jnp.float32,
        )
        weighted_ref[:, tile] = (x_ref[:, tile].astype(jnp.float32) * spread).astype(jnp.bfloat16)
    for copy in copies:
        copy.wait()


def first_rows(source_ref, halo, weight, bias, start_ref, padded_ref):
    padded_ref[0:8, :] = halo.astype(jnp.float32)
    padded_ref[8:, :] = source_ref[0:8, :].astype(jnp.float32)
    relative = lax.broadcasted_iota(jnp.int32, (8, LANES), 0)
    return convolve(padded_ref, weight, bias, relative, start_ref[0:8, :])


def states_kernel(
    b_ref, halo_ref, taps_ref, taps_bias_ref, start_ref, b_early_ref, weighted_ref, factor_ref,
    pieces_ref, b_conv_ref, padded_ref,
):
    state, features = b_ref.shape[1], weighted_ref.shape[1]
    members, rows, _ = pieces_ref.shape
    first = first_rows(
        b_ref, halo_ref[:, 0:state], taps_ref[:, 0:state], taps_bias_ref[:, 0:state], start_ref,
        padded_ref,
    )
    b_conv = jnp.concatenate([first.astype(jnp.float32), b_early_ref[8:, :]], axis=0)
    b_conv_ref[...] = b_conv.astype(jnp.bfloat16)
    b_rows = b_conv.T.astype(jnp.bfloat16)
    for j in range(features // 256):
        tile = slice(j * 256, (j + 1) * 256)
        end_state = jnp.dot(b_rows, weighted_ref[:, tile], preferred_element_type=jnp.float32)
        for m in range(members):
            pieces_ref[m, :, tile] = end_state[m * rows : (m + 1) * rows, :]
    spread = jnp.broadcast_to(factor_ref[...], (rows, LANES))
    for m in range(members):
        pieces_ref[m, :, features:] = spread


def prefix_kernel(
    heads, pieces_ref, before_ref, factors_ref, total_a_ref, total_b_ref, total_c_ref, single_ref,
    wide_ref,
):
    members, rows, padded = pieces_ref.shape
    features = padded - LANES
    for m in range(members):
        single_ref[m : m + 1, :] = pieces_ref[m, 0:1, features:]
    spread_rows(single_ref[...], features, heads, wide_ref)
    product = jnp.ones((1, LANES), jnp.float32)
    for m in range(members):
        factors_ref[m : m + 1, :] = product
        product = product * single_ref[m : m + 1, :]
    total = jnp.zeros((rows, features), jnp.float32)
    for m in range(members):
        before_ref[m] = total
        total = wide_ref[m : m + 1, :] * total + pieces_ref[m, :, 0:features]
    for total_ref in (total_a_ref, total_b_ref, total_c_ref):
        total_ref[:, 0:features] = total
        total_ref[:, features:] = jnp.broadcast_to(product, (rows, LANES))


def wide_factor(pair_ref, features, width):
    factor = pair_ref[0:1, features:]
    return jnp.concatenate(
        [tile_of_heads(factor, j, width) for j in range(features // LANES)], axis=1
    )


def states_in_kernel(heads, *refs):
    sent_near_ref, sent_far_ref, mixed_ref, before_ref, wide_ref, state_ref, near_ref = refs
    members, _, features = before_ref.shape
    second = lax.axis_index(OUTER) == 1
    mixed = mixed_ref[...]
    near_ref[...] = sent_near_ref[...] + jnp.where(second, mixed, 0.0)
    far = sent_far_ref[:, 0:features] + jnp.where(second, 0.0, mixed[:, 0:features])
    factor = wide_factor(near_ref, features, features // heads)
    entering = factor * far + near_ref[:, 0:features]
    for m in range(members):
        state_ref[m] = (wide_ref[m : m + 1, :] * entering + before_ref[m]).astype(jnp.bfloat16)


def products_of(
    c_ref, halo_ref, taps_ref, taps_bias_ref, start_ref, b_conv_ref, c_conv_ref, products_ref,
    padded_ref,
):
    tokens, state = c_ref.shape
    padded_ref[0:8, :] = halo_ref[:, state:].astype(jnp.float32)
    padded_ref[8:, :] = c_ref[...].astype(jnp.float32)
    relative = lax.broadcasted_iota(jnp.int32, (tokens, LANES), 0)
    c_conv = convolve(
        padded_ref, taps_ref[:, state:], taps_bias_ref[:, state:], relative, start_ref[...]
    )
    c_conv_ref[...] = c_conv
    products = lax.dot_general(
        c_conv, b_conv_ref[...], (((1,), (1,)), ((), ())), preferred_element_type=jnp.float32
    )
    row = lax.broadcasted_iota(jnp.int32, (tokens, tokens), 0)
    col = lax.broadcasted_iota(jnp.int32, (tokens, tokens), 1)
    starts = jnp.concatenate([start_ref[...]] * (tokens // LANES), axis=1)
    products_ref[...] = jnp.where((col <= row) & (col >= starts), products, 0.0)


def diagonal_of(
    start_ref, columns_ref, cum_rows_ref, step_rows_ref, x_ref, gate_ref, products_ref, gated_ref,
    scale_ref,
):
    tokens, features = x_ref.shape
    width, half = features // cum_rows_ref.shape[0], tokens // 2
    columns = columns_ref[...]
    carried = jnp.where(start_ref[...] < 0, jnp.exp(columns), 0.0)
    lane = lax.broadcasted_iota(jnp.int32, (tokens, LANES), 1)
    per = LANES // width
    for j in range(features // LANES):
        tile = slice(j * LANES, (j + 1) * LANES)
        diagonal = None
        for k in range(per):
            h = j * per + k
            column = jnp.broadcast_to(columns[:, h : h + 1], (tokens, LANES))
            cum_row, step_row = cum_rows_ref[h : h + 1, :], step_rows_ref[h : h + 1, :]
            upper = (
                products_ref[0:half, 0:half] * jnp.exp(column[0:half] - cum_row[:, 0:half])
            ) * step_row[:, 0:half]
            lower_left = (
                products_ref[half:, 0:half] * jnp.exp(column[half:] - cum_row[:, 0:half])
            ) * step_row[:, 0:half]
            lower_right = (
                products_ref[half:, half:] * jnp.exp(column[half:] - cum_row[:, half:])
            ) * step_row[:, half:]
            lower = jnp.concatenate([lower_left, lower_right], axis=1).astype(jnp.bfloat16)
            part = jnp.concatenate(
                [
                    jnp.dot(upper.astype(jnp.bfloat16), x_ref[0:half, tile],
                            preferred_element_type=jnp.float32),
                    jnp.dot(lower, x_ref[:, tile], preferred_element_type=jnp.float32),
                ],
                axis=0,
            )
            diagonal = part if diagonal is None else jnp.where(lane < k * width, diagonal, part)
        gate = gate_ref[:, tile].astype(jnp.float32)
        gate = gate * jax.nn.sigmoid(gate)
        gated_ref[:, tile] = diagonal * gate
        scale_ref[:, tile] = tile_of_heads(carried, j, width) * gate


def diagonal_kernel(turn, *refs):
    (*sources, columns_ref, cum_rows_ref, step_rows_ref, x_ref, gate_ref, factors_ref) = refs[:12]
    wide_ref, c_conv_ref, gated_ref, scale_ref, products_ref, padded_ref = refs[-6:]
    place = lax.axis_index(OUTER)

    @pl.when((place == 0, place == 1, place >= 2)[turn])
    def _():
        spread_rows(factors_ref[...], x_ref.shape[1], cum_rows_ref.shape[0], wide_ref)
        products_of(*sources, c_conv_ref, products_ref, padded_ref)
        diagonal_of(
            sources[4], columns_ref, cum_rows_ref, step_rows_ref, x_ref, gate_ref, products_ref,
            gated_ref, scale_ref,
        )


def gate_kernel(state_ref, c_conv_ref, diagonal_ref, scale_ref, gated_ref, squares_ref):
    members, rows, features = state_ref.shape
    c_conv = c_conv_ref[...]
    squares = jnp.zeros((c_conv.shape[0], LANES), jnp.float32)
    for j in range(features // LANES):
        tile = slice(j * LANES, (j + 1) * LANES)
        state = state_ref[:, :, tile].astype(jnp.float32).reshape(members * rows, LANES)
        carried = jnp.dot(c_conv, state.astype(jnp.bfloat16), preferred_element_type=jnp.float32)
        gated = diagonal_ref[:, tile] + scale_ref[:, tile] * carried
        gated_ref[:, tile] = gated
        squares = squares + gated * gated
    ones = jnp.ones((8, LANES), jnp.bfloat16)
    squares_ref[...] = sum(
        lax.dot_general(ones, part, (((1,), (1,)), ((), ())), preferred_element_type=jnp.float32)
        for part in reversed(bf16_parts(squares))
    )[0:1]


def normalize_kernel(features_all, squares_ref, gated_ref, gain_ref, out_ref, rows_ref, sems):
    count = squares_ref.shape[0]
    tokens, features = gated_ref.shape
    total = squares_ref[0]
    for k in range(1, count):
        total = total + squares_ref[k]
    scale = lax.rsqrt(total / features_all + epsilon)
    scale = jnp.broadcast_to(scale, (LANES, tokens)).T
    chunks = sems.shape[0]
    size = tokens // chunks
    copies = []
    for i in range(chunks):
        part = slice(i * size, (i + 1) * size)
        for j in range(features // LANES):
            tile = slice(j * LANES, (j + 1) * LANES)
            rows_ref[part, tile] = (
                gated_ref[part, tile] * scale[part] * gain_ref[j : j + 1, :]
            ).astype(jnp.bfloat16)
        copies.append(
            pltpu.make_async_copy(
                rows_ref.at[pl.ds(i * size, size), :], out_ref.at[pl.ds(i * size, size), :],
                sems.at[i],
            )
        )
        copies[-1].start()
    for copy in copies:
        copy.wait()


def body(
    inputs, gate_input, b_source, c_source, step_raw, step_bias, decay_rate, conv_weight,
    conv_bias, norm_gain, doc_lengths,
):
    tokens, features = inputs.shape
    heads = step_raw.shape[1]
    state = b_source.shape[1]
    members = 1
    for axis in GROUP:
        members *= lax.axis_size(axis)
    outer = lax.axis_size(OUTER)
    rows = state // members
    shards = members * outer
    ahead = lambda n, k: [(i, i + k) for i in range(n - k)]

    bf16 = jnp.bfloat16
    small = [
        doc_lengths[None, :], step_raw.T, step_bias[None, :], decay_rate[None, :], b_source,
        conv_weight, conv_bias[None, :],
    ]
    tails, *small = call(
        tails_kernel,
        [out((8, 2 * state), bf16)] + [out(o.shape, o.dtype) for o in small],
        b_source, c_source, *small,
        hbm=2 + len(small), scratch=[pltpu.SemaphoreType.DMA((2 + len(small),))],
        flops=20_000_000_000,
    )
    halo = lax.ppermute(tails, SEQ, ahead(shards, 1))
    operands = [
        c_source, norm_gain.reshape(features // LANES, LANES),
    ]
    results = call(
        prepare_kernel,
        [out(o.shape, o.dtype) for o in operands]
        + [
            out((tokens, features), bf16), out((heads, tokens)), out((heads, tokens)),
            out((tokens, LANES)), out((1, LANES)), out((tokens, LANES), jnp.int32),
            out((tokens, state)),
        ],
        *operands, inputs, *small, tails,
        hbm=len(operands),
        scratch=[
            pltpu.VMEM((LANES, tokens), jnp.float32),
            pltpu.VMEM((tokens + 8, state), jnp.float32),
            pltpu.SemaphoreType.DMA((len(operands),)),
        ],
    )
    b, taps, taps_bias = small[4:]
    c, gain = results[0:2]
    weighted, cum_rows, step_rows, columns, factor, start, b_early = results[2:]
    pieces, b_conv = call(
        states_kernel,
        [out((members, rows, features + LANES)), out((tokens, state), bf16)],
        b, halo, taps, taps_bias, start, b_early, weighted, factor,
        scratch=[pltpu.VMEM((16, state), jnp.float32)],
    )
    pieces = lax.all_to_all(pieces, GROUP, 0, 0)
    pair = out((rows, features + LANES))
    before, factors, total_a, total_b, total_c = call(
        functools.partial(prefix_kernel, heads),
        [out((members, rows, features)), out((members, LANES)), pair, pair, pair],
        pieces,
        scratch=[
            pltpu.VMEM((members, LANES), jnp.float32),
            pltpu.VMEM((members, features), jnp.float32),
        ],
    )

    def diagonal_terms(turn, token, *before):
        sources = [
            c, halo, taps, taps_bias, start, b_conv, columns, cum_rows, step_rows, inputs, gate_input,
            factors,
        ]
        token = [] if token is None else [token]
        count = len(sources)
        return call(
            functools.partial(diagonal_kernel, turn),
            [out(t.shape) for t in token] + [
                out((members, features)), out((tokens, state), bf16), out((tokens, features)),
                out((tokens, features)),
            ],
            *sources, *token, *before, flops=20_000_000_000,
            aliases={count + k: k for k in range(len(token) + len(before))},
            scratch=[
                pltpu.VMEM((tokens, tokens), jnp.float32),
                pltpu.VMEM((tokens + 8, state), jnp.float32),
            ],
        )

    def send(total, *pairs):
        return lax.ppermute(total, OUTER, pairs)

    total_a, *diagonal = diagonal_terms(0, total_a)
    far = send(total_a, (0, 2))
    total_b, *diagonal = diagonal_terms(1, total_b, *diagonal)
    mixed = send(total_b, (0, 1), (1, 3))
    near = send(total_c, (1, 2), (2, 3))
    wide, c_conv, diagonal, scale = diagonal_terms(2, None, *diagonal)
    states_in = call(
        functools.partial(states_in_kernel, heads),
        out((members, rows, features), bf16),
        near, far, mixed, before, wide,
        scratch=[pltpu.VMEM(pair.shape, jnp.float32)],
    )
    states_in = lax.all_to_all(states_in, GROUP, 0, 0)
    gated, squares = call(
        gate_kernel,
        [out((tokens, features)), out((1, tokens))],
        states_in, c_conv, diagonal, scale,
    )
    squares = lax.all_gather(squares, "tp")
    return call(
        functools.partial(normalize_kernel, features * lax.axis_size("tp")),
        jax.ShapeDtypeStruct((tokens, features), bf16),
        squares, gated, gain, to_hbm=True,
        scratch=[pltpu.VMEM((tokens, features), bf16), pltpu.SemaphoreType.DMA((4,))],
    )


def solution(mesh):
    finer = Mesh(
        mesh.devices.reshape(4, 2, 4, 4, mesh.shape["tp"]), ("za", "zb", "y", "x", "tp")
    )
    in_specs = (
        P(SEQ, "tp"), P(SEQ, "tp"), P(SEQ, None), P(SEQ, None), P(SEQ, "tp"), P("tp"), P("tp"),
        P(), P(), P("tp"), P(),
    )
    return jax.shard_map(
        body, mesh=finer, in_specs=in_specs, out_specs=P(SEQ, "tp"), check_vma=False
    )
```

profile of v0, /device:TPU:1, one launch (start us, length us, event | category | flops | bytes accessed | tf_op | source)
XLA Modules:
  0.0 75.6 jit_solution(11577418158969915240)
XLA Ops:
  0.0 0.0 copy-start
  0.0 1.1 %shard_map.109 = (bf16[8,256]{1,0:T(8,128)(2,1)S(1)}, s32[1,8]{1,0:T(1,128)S(1)}, f32[20,256]{1,0:T(8,128)S(1)}, f32[1,20]{1,0:T(1,128)S(1)}, f32[1,20]{1,0:T(1,...) custom-call(bf16[256,128]{1,0:T(8,128)(2,1)} %refs_4_.1, ...), custom_call_target="tpu_custom_call" | custom-call | flops 20000000000 | bytes 1000000 | tf_op jit(solution)/shard_map/pallas_call | solution.py:27
  1.1 3.9 %collective-permute-start = (bf16[8,256]{1,0:T(8,128)(2,1)S(1)}, bf16[8,256]{1,0:T(8,128)(2,1)S(1)}, u32[]{:S(2)}, u32[]{:S(2)}) collective-permute-start(bf16[8,256]{1,0:T(8,128)(2,1)S(1)} %get-tuple-element.46.refs_10_), channel_id=1, source_target_pairs={{0,4},{4,8},{8,12},{12,16},{16,20},{20,24},{24,28},{28,32},{32,36}... | collective-permute-start | bytes 12296 | tf_op jit(solution)/shard_map/ppermute | solution.py:425
  5.0 0.0 copy-done
  5.0 1.1 %shard_map.110 = (bf16[256,128]{1,0:T(8,128)(2,1)S(1)}, f32[10,128]{1,0:T(8,128)S(1)}, bf16[256,1280]{1,0:T(8,128)(2,1)S(1)}, f32[20,256]{1,0:T(8,128)S(1)}, f32...) custom-call(bf16[256,128]{1,0:T(8,128)(2,1)} %refs_0_.1, ...), custom_call_target="tpu_custom_call" | custom-call | flops 1000000 | bytes 1000000 | tf_op jit(solution)/shard_map/pallas_call | solution.py:27
  6.2 0.0 collective-permute-done.halo_ref.refs_1_
  6.2 0.3 shard_map.111
  6.5 0.0 copy-start.1
  6.5 18.8 %all_to_all.10.pieces_ref = f32[32,4,1408]{2,1,0:T(4,128)S(1)} all-to-all(f32[32,4,1408]{2,1,0:T(4,128)S(1)} %get-tuple-element.57), channel_id=1, replica_groups=mesh['za'=4,'zb'=2,'y'=4,'x'=4,'tp'=4] {'zb','y','x'}, dimensions={0} | all-to-all | bytes 1441792 | tf_op jit(solution)/shard_map/all_to_all | solution.py:454
  25.3 0.4 shard_map.112
  25.8 0.7 collective-permute-start.1
  26.4 0.0 copy-done.1
  26.4 1.8 %shard_map.113 = (f32[4,1408]{1,0:T(4,128)S(1)}, f32[32,1280]{1,0:T(8,128)S(1)}, bf16[256,128]{1,0:T(8,128)(2,1)S(1)}, f32[256,1280]{1,0:T(8,128)S(1)}, f32[256,1280]{1,0:T(8,128)S(1)}) custom-call(bf16[256,128]{1,0:T(8,128)(2,1)S(1)} %get-tuple-element.59.refs_0_, ...), custom_call_target="tpu_custom_call", output_to_operand_aliasing={{0}: (12, {})} | custom-call | flops 20000000000 | bytes 1000000 | tf_op jit(solution)/shard_map/pallas_call | solution.py:27
  28.2 11.3 %collective-permute-start.2 = (f32[4,1408]{1,0:T(4,128)S(1)}, f32[4,1408]{1,0:T(4,128)S(1)}, u32[]{:S(2)}, u32[]{:S(2)}) collective-permute-start(f32[4,1408]{1,0:T(4,128)S(1)} %get-tuple-element.66), channel_id=1, source_target_pairs={{0,256},{1,257},{2,258},{3,259},{4,260},{5,261},{6,262},{7,263},{8... | collective-permute-start | bytes 67592 | tf_op jit(solution)/shard_map/ppermute | solution.py:488
  39.6 1.3 %collective-permute-start.3 = (f32[4,1408]{1,0:T(4,128)S(1)}, f32[4,1408]{1,0:T(4,128)S(1)}, u32[]{:S(2)}, u32[]{:S(2)}) collective-permute-start(f32[4,1408]{1,0:T(4,128)S(1)} %get-tuple-element.72), channel_id=1, source_target_pairs={{0,128},{128,384},{1,129},{129,385},{2,130},{130,386},{3,131},{131... | collective-permute-start | bytes 67592 | tf_op jit(solution)/shard_map/ppermute | solution.py:488
  40.9 0.0 collective-permute-done.1.refs_0_
  40.9 0.0 collective-permute-done.2.refs_1_
  40.9 0.9 %collective-permute-done.3.refs_2_ = f32[4,1408]{1,0:T(4,128)S(1)} collective-permute-done((f32[4,1408]{1,0:T(4,128)S(1)}, f32[4,1408]{1,0:T(4,128)S(1)}, u32[]{:S(2)}, u32[]{:S(2)}) %collective-permute-start.3) | collective-permute-done | bytes 22560 | tf_op jit(solution)/shard_map/ppermute | solution.py:488
  41.8 0.3 shard_map.116
  42.1 13.6 %all_to_all.11.state_ref = bf16[32,4,1280]{2,1,0:T(4,128)(2,1)S(1)} all-to-all(bf16[32,4,1280]{2,1,0:T(4,128)(2,1)S(1)} %shard_map.116), channel_id=1, replica_groups=mesh['za'=4,'zb'=2,'y'=4,'x'=4,'tp'=4] {'zb','y','x'}, dimensions={0} | all-to-all | bytes 655360 | tf_op jit(solution)/shard_map/all_to_all | solution.py:502
  55.7 0.6 shard_map.117
  56.2 18.4 %all-gather.1.squares_ref = f32[4,1,256]{2,1,0:T(1,128)S(1)} all-gather(f32[1,1,256]{2,1,0:T(1,128)S(1)} %bitcast.7), channel_id=2, replica_groups=mesh['za'=4,'zb'=2,'y'=4,'x'=4,'tp'=4] {'tp'}, dimensions={0}, use_global_device_ids=true | all-gather | bytes 5120 | tf_op jit(solution)/shard_map/all_gather | solution.py:508
  74.6 1.0 %shard_map.118 = bf16[256,1280]{1,0:T(8,128)(2,1)} custom-call(f32[4,1,256]{2,1,0:T(1,128)S(1)} %all-gather.1.squares_ref, f32[256,1280]{1,0:T(8,128)S(1)} %get-tuple-element.83.gated_ref, f32[10,128]{1,0:T(8,128)S(1)} %get-tuple-element.84.gain_ref), custom_call_target="tpu_custom_call" | custom-call | flops 1000000 | bytes 1000000 | tf_op jit(solution)/shard_map/pallas_call | solution.py:27
  (2 shorter events, 0.0 us)
Async XLA Ops:
  0.0 5.0 %copy-start = (bf16[256,1280]{1,0:T(8,128)(2,1)S(1)}, bf16[256,1280]{1,0:T(8,128)(2,1)}, u32[]{:S(2)}) copy-start(bf16[256,1280]{1,0:T(8,128)(2,1)} %refs_9_.5) | copy-start | bytes 1966084
  1.1 5.1 %collective-permute-start = (bf16[8,256]{1,0:T(8,128)(2,1)S(1)}, bf16[8,256]{1,0:T(8,128)(2,1)S(1)}, u32[]{:S(2)}, u32[]{:S(2)}) collective-permute-start(bf16[8,256]{1,0:T(8,128)(2,1)S(1)} %get-tuple-element.46.refs_10_), channel_id=1, source_target_pairs={{0,4},{4,8},{8,12},{12,16},{16,20},{20,24},{24,28},{28,32},{32,36}... | collective-permute-start | bytes 12296 | tf_op jit(solution)/shard_map/ppermute | solution.py:425
  6.5 19.9 %copy-start.1 = (bf16[256,1280]{1,0:T(8,128)(2,1)S(1)}, bf16[256,1280]{1,0:T(8,128)(2,1)}, u32[]{:S(2)}) copy-start(bf16[256,1280]{1,0:T(8,128)(2,1)} %refs_10_.5) | copy-start | bytes 1966084
  25.8 15.1 %collective-permute-start.1 = (f32[4,1408]{1,0:T(4,128)S(1)}, f32[4,1408]{1,0:T(4,128)S(1)}, u32[]{:S(2)}, u32[]{:S(2)}) collective-permute-start(f32[4,1408]{1,0:T(4,128)S(1)} %get-tuple-element.58), channel_id=1, source_target_pairs={{128,256},{256,384},{129,257},{257,385},{130,258},{258,386},{131,2... | collective-permute-start | bytes 67592 | tf_op jit(solution)/shard_map/ppermute | solution.py:488
  28.2 12.7 %collective-permute-start.2 = (f32[4,1408]{1,0:T(4,128)S(1)}, f32[4,1408]{1,0:T(4,128)S(1)}, u32[]{:S(2)}, u32[]{:S(2)}) collective-permute-start(f32[4,1408]{1,0:T(4,128)S(1)} %get-tuple-element.66), channel_id=1, source_target_pairs={{0,256},{1,257},{2,258},{3,259},{4,260},{5,261},{6,262},{7,263},{8... | collective-permute-start | bytes 67592 | tf_op jit(solution)/shard_map/ppermute | solution.py:488
  39.6 2.2 %collective-permute-start.3 = (f32[4,1408]{1,0:T(4,128)S(1)}, f32[4,1408]{1,0:T(4,128)S(1)}, u32[]{:S(2)}, u32[]{:S(2)}) collective-permute-start(f32[4,1408]{1,0:T(4,128)S(1)} %get-tuple-element.72), channel_id=1, source_target_pairs={{0,128},{128,384},{1,129},{129,385},{2,130},{130,386},{3,131},{131... | collective-permute-start | bytes 67592 | tf_op jit(solution)/shard_map/ppermute | solution.py:488
where the time goes:
time: 75.9 us; the launch traced here: 75.6 us
  blocking collectives  50.8 us (67%)
  starting transfers between devices  17.2 us (23%)
  Pallas kernels  6.65 us (9%)
  waiting for transfers between devices  0.87 us (1%)
    all_to_all x1, blocking collectives, body(): pieces = lax.all_to_all(pieces, GROUP, 0, 0)  18.8 us
    all_gather x1, blocking collectives, body(): squares = lax.all_gather(squares, 'tp')  18.4 us
    all_to_all x1, blocking collectives, body(): states_in = lax.all_to_all(states_in, GROUP, 0, 0)  13.6 us
    ppermute x3, starting transfers between devices, send(): return lax.ppermute(total, OUTER, pairs)  13.2 us
    pallas_call x10, Pallas kernels, call(): pl.pallas_call(kernel, out_shape=list(outs) if multiple else outs, in_spe...  6.65 us
    ppermute x1, starting transfers between devices, body(): halo = lax.ppermute(tails, SEQ, ahead(shards, 1))  3.93 us
  transfers between devices with their start and end apart: 4, of which 1 were waited for; matrix products, arithmetic and copies ran while one was open for 0% of the time, Pallas kernels for 4%

commit v1 on v0

--- a/solution.py
+++ b/solution.py
@@ -63,8 +63,8 @@
     ]
     for k, (source, target) in enumerate(zip(sources, targets)):
         copies.append(pltpu.make_async_copy(source, target, sems.at[k + 2]))
-    for copy in copies:
-        copy.start()
+    for k, copy in enumerate(copies):
+        copy.start(priority=1 if k < 2 else 0)
     for copy in copies:
         copy.wait()
 
@@ -258,14 +258,11 @@
 
 
 def states_in_kernel(heads, *refs):
-    sent_near_ref, sent_far_ref, mixed_ref, before_ref, wide_ref, state_ref, near_ref = refs
+    *near_refs, far_ref, before_ref, wide_ref, state_ref, near_ref = refs
     members, _, features = before_ref.shape
-    second = lax.axis_index(OUTER) == 1
-    mixed = mixed_ref[...]
-    near_ref[...] = sent_near_ref[...] + jnp.where(second, mixed, 0.0)
-    far = sent_far_ref[:, 0:features] + jnp.where(second, 0.0, mixed[:, 0:features])
+    near_ref[...] = sum(ref[...] for ref in near_refs)
     factor = wide_factor(near_ref, features, features // heads)
-    entering = factor * far + near_ref[:, 0:features]
+    entering = factor * far_ref[:, 0:features] + near_ref[:, 0:features]
     for m in range(members):
         state_ref[m] = (wide_ref[m : m + 1, :] * entering + before_ref[m]).astype(jnp.bfloat16)
 
@@ -488,15 +485,15 @@
         return lax.ppermute(total, OUTER, pairs)
 
     total_a, *diagonal = diagonal_terms(0, total_a)
-    far = send(total_a, (0, 2))
+    near_a = send(total_a, (0, 1))
     total_b, *diagonal = diagonal_terms(1, total_b, *diagonal)
-    mixed = send(total_b, (0, 1), (1, 3))
-    near = send(total_c, (1, 2), (2, 3))
+    far = send(total_b, (0, 2), (1, 3))
+    near_b = send(total_c, (1, 2), (2, 3))
     wide, c_conv, diagonal, scale = diagonal_terms(2, None, *diagonal)
     states_in = call(
         functools.partial(states_in_kernel, heads),
         out((members, rows, features), bf16),
-        near, far, mixed, before, wide,
+        near_a, near_b, far, before, wide,
         scratch=[pltpu.VMEM(pair.shape, jnp.float32)],
     )
     states_in = lax.all_to_all(states_in, GROUP, 0, 0)

time: 75.9 us -> 75.2 us (level)
  no operation moved by 1% of the time
where the time goes in v1:
time: 75.2 us; the launch traced here: 74.9 us
  blocking collectives  50.8 us (68%)
  starting transfers between devices  16.5 us (22%)
  Pallas kernels  6.61 us (9%)
  waiting for transfers between devices  0.87 us (1%)
    all_to_all x1, blocking collectives, body(): pieces = lax.all_to_all(pieces, GROUP, 0, 0)  18.8 us
    all_gather x1, blocking collectives, body(): squares = lax.all_gather(squares, 'tp')  18.4 us
    all_to_all x1, blocking collectives, body(): states_in = lax.all_to_all(states_in, GROUP, 0, 0)  13.6 us
    ppermute x3, starting transfers between devices, send(): return lax.ppermute(total, OUTER, pairs)  12.6 us
    pallas_call x10, Pallas kernels, call(): pl.pallas_call(kernel, out_shape=list(outs) if multiple else outs, in_spe...  6.61 us
    ppermute x1, starting transfers between devices, body(): halo = lax.ppermute(tails, SEQ, ahead(shards, 1))  3.93 us
  transfers between devices with their start and end apart: 4, of which 1 were waited for; matrix products, arithmetic and copies ran while one was open for 0% of the time, Pallas kernels for 4%

profile of v1, /device:TPU:1, one launch (start us, length us, event | category | flops | bytes accessed | tf_op | source)
XLA Modules:
  0.0 74.9 jit_solution(15598339184328752624)
XLA Ops:
  0.0 0.0 copy-start
  0.0 1.1 %shard_map.109 = (bf16[8,256]{1,0:T(8,128)(2,1)S(1)}, s32[1,8]{1,0:T(1,128)S(1)}, f32[20,256]{1,0:T(8,128)S(1)}, f32[1,20]{1,0:T(1,128)S(1)}, f32[1,20]{1,0:T(1,...) custom-call(bf16[256,128]{1,0:T(8,128)(2,1)} %refs_4_.1, ...), custom_call_target="tpu_custom_call" | custom-call | flops 20000000000 | bytes 1000000 | tf_op jit(solution)/shard_map/pallas_call | solution.py:27
  1.1 3.9 %collective-permute-start = (bf16[8,256]{1,0:T(8,128)(2,1)S(1)}, bf16[8,256]{1,0:T(8,128)(2,1)S(1)}, u32[]{:S(2)}, u32[]{:S(2)}) collective-permute-start(bf16[8,256]{1,0:T(8,128)(2,1)S(1)} %get-tuple-element.52.refs_10_), channel_id=1, source_target_pairs={{0,4},{4,8},{8,12},{12,16},{16,20},{20,24},{24,28},{28,32},{32,36}... | collective-permute-start | bytes 12296 | tf_op jit(solution)/shard_map/ppermute | solution.py:422
  5.0 0.0 copy-done
  5.0 1.1 %shard_map.110 = (bf16[256,128]{1,0:T(8,128)(2,1)S(1)}, f32[10,128]{1,0:T(8,128)S(1)}, bf16[256,1280]{1,0:T(8,128)(2,1)S(1)}, f32[20,256]{1,0:T(8,128)S(1)}, f32...) custom-call(bf16[256,128]{1,0:T(8,128)(2,1)} %refs_0_.1, ...), custom_call_target="tpu_custom_call" | custom-call | flops 1000000 | bytes 1000000 | tf_op jit(solution)/shard_map/pallas_call | solution.py:27
  6.1 0.0 collective-permute-done.halo_ref.refs_1_
  6.2 0.3 shard_map.111
  6.5 0.0 copy-start.1
  6.5 18.8 %all_to_all.10.pieces_ref = f32[32,4,1408]{2,1,0:T(4,128)S(1)} all-to-all(f32[32,4,1408]{2,1,0:T(4,128)S(1)} %get-tuple-element.62), channel_id=1, replica_groups=mesh['za'=4,'zb'=2,'y'=4,'x'=4,'tp'=4] {'zb','y','x'}, dimensions={0} | all-to-all | bytes 1441792 | tf_op jit(solution)/shard_map/all_to_all | solution.py:451
  25.3 0.4 shard_map.112
  25.7 0.7 collective-permute-start.2
  26.4 0.0 copy-done.1
  26.4 1.8 %shard_map.113 = (f32[4,1408]{1,0:T(4,128)S(1)}, f32[32,1280]{1,0:T(8,128)S(1)}, bf16[256,128]{1,0:T(8,128)(2,1)S(1)}, f32[256,1280]{1,0:T(8,128)S(1)}, f32[256,1280]{1,0:T(8,128)S(1)}) custom-call(bf16[256,128]{1,0:T(8,128)(2,1)S(1)} %get-tuple-element.53.refs_0_, ...), custom_call_target="tpu_custom_call", output_to_operand_aliasing={{0}: (12, {})} | custom-call | flops 20000000000 | bytes 1000000 | tf_op jit(solution)/shard_map/pallas_call | solution.py:27
  28.2 9.2 %collective-permute-start.1 = (f32[4,1408]{1,0:T(4,128)S(1)}, f32[4,1408]{1,0:T(4,128)S(1)}, u32[]{:S(2)}, u32[]{:S(2)}) collective-permute-start(f32[4,1408]{1,0:T(4,128)S(1)} %get-tuple-element.65), channel_id=1, source_target_pairs={{0,128},{1,129},{2,130},{3,131},{4,132},{5,133},{6,134},{7,135},{8... | collective-permute-start | bytes 67592 | tf_op jit(solution)/shard_map/ppermute | solution.py:485
  37.5 2.7 %collective-permute-start.3 = (f32[4,1408]{1,0:T(4,128)S(1)}, f32[4,1408]{1,0:T(4,128)S(1)}, u32[]{:S(2)}, u32[]{:S(2)}) collective-permute-start(f32[4,1408]{1,0:T(4,128)S(1)} %get-tuple-element.72), channel_id=1, source_target_pairs={{0,256},{128,384},{1,257},{129,385},{2,258},{130,386},{3,259},{131... | collective-permute-start | bytes 67592 | tf_op jit(solution)/shard_map/ppermute | solution.py:485
  40.2 0.0 collective-permute-done.2.refs_1_
  40.2 0.0 collective-permute-done.1.refs_0_
  40.2 0.9 %collective-permute-done.3.refs_2_ = f32[4,1408]{1,0:T(4,128)S(1)} collective-permute-done((f32[4,1408]{1,0:T(4,128)S(1)}, f32[4,1408]{1,0:T(4,128)S(1)}, u32[]{:S(2)}, u32[]{:S(2)}) %collective-permute-start.3) | collective-permute-done | bytes 22560 | tf_op jit(solution)/shard_map/ppermute | solution.py:485
  41.1 0.3 shard_map.116
  41.4 13.6 %all_to_all.11.state_ref = bf16[32,4,1280]{2,1,0:T(4,128)(2,1)S(1)} all-to-all(bf16[32,4,1280]{2,1,0:T(4,128)(2,1)S(1)} %shard_map.116), channel_id=1, replica_groups=mesh['za'=4,'zb'=2,'y'=4,'x'=4,'tp'=4] {'zb','y','x'}, dimensions={0} | all-to-all | bytes 655360 | tf_op jit(solution)/shard_map/all_to_all | solution.py:499
  55.0 0.6 shard_map.117
  55.6 18.4 %all-gather.1.squares_ref = f32[4,1,256]{2,1,0:T(1,128)S(1)} all-gather(f32[1,1,256]{2,1,0:T(1,128)S(1)} %bitcast.7), channel_id=2, replica_groups=mesh['za'=4,'zb'=2,'y'=4,'x'=4,'tp'=4] {'tp'}, dimensions={0}, use_global_device_ids=true | all-gather | bytes 5120 | tf_op jit(solution)/shard_map/all_gather | solution.py:505
  73.9 1.0 %shard_map.118 = bf16[256,1280]{1,0:T(8,128)(2,1)} custom-call(f32[4,1,256]{2,1,0:T(1,128)S(1)} %all-gather.1.squares_ref, f32[256,1280]{1,0:T(8,128)S(1)} %get-tuple-element.83.gated_ref, f32[10,128]{1,0:T(8,128)S(1)} %get-tuple-element.84.gain_ref), custom_call_target="tpu_custom_call" | custom-call | flops 1000000 | bytes 1000000 | tf_op jit(solution)/shard_map/pallas_call | solution.py:27
  (2 shorter events, 0.0 us)
Async XLA Ops:
  0.0 5.0 %copy-start = (bf16[256,1280]{1,0:T(8,128)(2,1)S(1)}, bf16[256,1280]{1,0:T(8,128)(2,1)}, u32[]{:S(2)}) copy-start(bf16[256,1280]{1,0:T(8,128)(2,1)} %refs_9_.5) | copy-start | bytes 1966084
  1.1 5.1 %collective-permute-start = (bf16[8,256]{1,0:T(8,128)(2,1)S(1)}, bf16[8,256]{1,0:T(8,128)(2,1)S(1)}, u32[]{:S(2)}, u32[]{:S(2)}) collective-permute-start(bf16[8,256]{1,0:T(8,128)(2,1)S(1)} %get-tuple-element.52.refs_10_), channel_id=1, source_target_pairs={{0,4},{4,8},{8,12},{12,16},{16,20},{20,24},{24,28},{28,32},{32,36}... | collective-permute-start | bytes 12296 | tf_op jit(solution)/shard_map/ppermute | solution.py:422
  6.5 19.9 %copy-start.1 = (bf16[256,1280]{1,0:T(8,128)(2,1)S(1)}, bf16[256,1280]{1,0:T(8,128)(2,1)}, u32[]{:S(2)}) copy-start(bf16[256,1280]{1,0:T(8,128)(2,1)} %refs_10_.5) | copy-start | bytes 1966084
  25.7 14.5 %collective-permute-start.2 = (f32[4,1408]{1,0:T(4,128)S(1)}, f32[4,1408]{1,0:T(4,128)S(1)}, u32[]{:S(2)}, u32[]{:S(2)}) collective-permute-start(f32[4,1408]{1,0:T(4,128)S(1)} %get-tuple-element.66), channel_id=1, source_target_pairs={{128,256},{256,384},{129,257},{257,385},{130,258},{258,386},{131,2... | collective-permute-start | bytes 67592 | tf_op jit(solution)/shard_map/ppermute | solution.py:485
  28.2 12.0 %collective-permute-start.1 = (f32[4,1408]{1,0:T(4,128)S(1)}, f32[4,1408]{1,0:T(4,128)S(1)}, u32[]{:S(2)}, u32[]{:S(2)}) collective-permute-start(f32[4,1408]{1,0:T(4,128)S(1)} %get-tuple-element.65), channel_id=1, source_target_pairs={{0,128},{1,129},{2,130},{3,131},{4,132},{5,133},{6,134},{7,135},{8... | collective-permute-start | bytes 67592 | tf_op jit(solution)/shard_map/ppermute | solution.py:485
  37.5 3.6 %collective-permute-start.3 = (f32[4,1408]{1,0:T(4,128)S(1)}, f32[4,1408]{1,0:T(4,128)S(1)}, u32[]{:S(2)}, u32[]{:S(2)}) collective-permute-start(f32[4,1408]{1,0:T(4,128)S(1)} %get-tuple-element.72), channel_id=1, source_target_pairs={{0,256},{128,384},{1,257},{129,385},{2,258},{130,386},{3,259},{131... | collective-permute-start | bytes 67592 | tf_op jit(solution)/shard_map/ppermute | solution.py:485
